TPU v7x, 32 devices: a whole 2x2x4 slice. The times are simulated.
32 devices in a mesh: lat: 16 (over z, y, x), lev: 2 (over core).
Axes of the slice: x: 2, y: 2, z: 4, core: 2. Of those that a mesh axis runs over, the one named last changes fastest.
Arguments:
- fields: float32 [160, 3, 16, 2560], P('lat', None, 'lev'), may hold values from 0.1 to 5
- lat_fraction: float32 [160], P('lat'), may hold values from 0 to 1
- lon_fraction: float32 [160], P('lat'), may hold values from 0 to 1
- lon_shift: int32 [160], P('lat'), may hold values from 0 to 2559
- departure_row: int32 [160], P('lat'), may hold values from 1 to 157, as said below
- extents: int32 [16, 2], P('lat'), may hold values from 1 to 4
Outputs:
- advected: float32 [160, 3, 16, 2560], P('lat', None, 'lev')
Inputs may be any that keep to these rules, and one draw needn't show every extreme that they name: departure_row[r] lies within 39 rows of r.
All inputs are finite; a program needn't handle non-finite values.
Results may differ from a plain program's by a relative error of at most 0.0003.
Values sent between devices are 32-bit elements; how exact they have to be, the bound alone decides.
A program may use at most 128 MiB of HBM per device.

v0:
```python
import functools
import math

import jax
import jax.numpy as jnp
import numpy as np
from jax import lax
from jax.experimental import pallas as pl
from jax.experimental.pallas import tpu as pltpu
from jax.sharding import PartitionSpec as P

REACH = 4
LANES = 128
DEPTH = 5
MESH = pl.DeviceIdType.MESH

UP = {
    0: [],
    1: [(0, 1), (0, 2), (0, 0)],
    2: [(0, 0), (0, 1), (0, 2), (1, 0)],
    3: [(1, 1), (1, 2), (1, 0), (0, 0)],
}
UP_OVER_ONE = {3: [(2, 0), (2, 1), (2, 2)], 2: [(1, 1), (1, 2)]}
UP_OVER_TWO = {3: [(0, 1), (0, 2)]}


def arrivals(member):
    def both(table):
        up = [(1, m, h) for m, h in table.get(member, [])]
        down = [(-1, 3 - m, h) for m, h in table.get(3 - member, [])]
        return up + down

    one = [(0, member ^ 1, h) for h in range(3)] + [(0, member ^ 3, 0)] + both(UP_OVER_ONE)
    two = [(0, member ^ 2, h) for h in range(3)] + [(0, member ^ 3, h) for h in (1, 2)] + both(UP_OVER_TWO)
    up = [(1, member, h) for h in range(3)] + [(1, m, h) for m, h in UP[member]]
    down = [(-1, member, h) for h in range(3)] + [(-1, 3 - m, h) for m, h in UP[3 - member]]
    return {"one": one, "two": two, "up": up, "down": down}


LINKS = ("one", "two", "up", "down")


def cubic(t):
    sixth = 1.0 / 6.0
    return (
        -t * (t - 1.0) * (t - 2.0) * sixth,
        (t + 1.0) * (t - 1.0) * (t - 2.0) * 0.5,
        -(t + 1.0) * t * (t - 2.0) * 0.5,
        (t + 1.0) * t * (t - 1.0) * sixth,
    )


def departure_of(row, first_row, rows, total_rows, departure_ref, extents_ref):
    low = first_row - extents_ref[0, 0] * rows + 1
    high = first_row + rows - 3 + extents_ref[0, 1] * rows
    inside = jnp.minimum(jnp.maximum(departure_ref[row], low), high)
    return jnp.minimum(jnp.maximum(inside, 1), total_rows - 3)


def exchange_kernel(bands, levs, lat_t_ref, lon_t_ref, departure_ref, extents_ref, area_ref, fields_ref,
                    halo_ref, table_ref, held, mine, met, sent, gathered, send_sem, recv_sem, local_sem,
                    table_send_sem, table_recv_sem):
    band, lev = lax.axis_index("lat"), lax.axis_index("lev")
    group, position = band // 4, lax.rem(band, 4)
    groups = bands // 4
    has_up = group < groups - 1
    has_down = group > 0
    rows, field_count = fields_ref.shape[:2]
    first_row, total_rows = band * rows, bands * rows
    step_one = 1 - 2 * lax.rem(position, 2)
    step_two = 2 - 4 * (position // 2)
    across = [{"lev": 1 - lev}, {"lat": band + step_one}, {"lat": band + step_two}]
    others = [{"lat": lax.rem(band + 4 * j, bands)} for j in range(1, groups)]

    barrier = pltpu.get_barrier_semaphore()
    for peer in across + others:
        pl.semaphore_signal(barrier, inc=1, device_id=peer, device_id_type=MESH)
    pl.semaphore_wait(barrier, len(across) + len(others))

    def cut(part):
        first = field_count * part // 3
        return pl.ds(first, field_count * (part + 1) // 3 - first)

    def halo_part(distance, part):
        slot = distance + 4 if distance < 0 else distance + 3
        return halo_ref.at[pl.ds(slot * rows, rows), cut(part)]

    def when(offset, body):
        if offset == 0:
            body()
        else:
            pl.when(has_up if offset == 1 else has_down)(body)

    came_over = [
        {item: (link, k) for link, items in arrivals(member).items() for k, item in enumerate(items)}
        for member in range(4)
    ]
    waited = [set() for _ in range(4)]

    def wait_for(member, item):
        if item in waited[member]:
            return
        waited[member].add(item)
        offset, m, h = item
        link, k = came_over[member][item]
        place = halo_part(4 * offset + m - member, h)
        when(
            offset,
            lambda: pltpu.make_async_remote_copy(
                src_ref=place, dst_ref=place,
                send_sem=send_sem.at[LINKS.index(link), k],
                recv_sem=recv_sem.at[LINKS.index(link), k],
                device_id={"lat": band}, device_id_type=MESH,
            ).wait_recv(),
        )

    def targets(member):
        return [
            ("up", member, -4, -1),
            ("down", member, 4, 1),
            ("one", member ^ 1, (member ^ 1) - member, 0),
            ("two", member ^ 2, (member ^ 2) - member, 0),
        ]

    def sends(member, k):
        for link, target, step, group_step in targets(member):
            items = arrivals(target)[link]
            if k < len(items):
                offset, m, h = items[k]
                here = offset + group_step
                own = here == 0 and m == member
                copy = pltpu.make_async_remote_copy(
                    src_ref=fields_ref.at[:, cut(h)] if own else halo_part(4 * here + m - member, h),
                    dst_ref=halo_part(4 * offset + m - target, h),
                    send_sem=send_sem.at[LINKS.index(link), k],
                    recv_sem=recv_sem.at[LINKS.index(link), k],
                    device_id={"lat": band + step}, device_id_type=MESH,
                )
                yield (None if own else (here, m, h)), (group_step if group_step else here), copy

    def on_each(body):
        for member in range(4):
            pl.when(position == member)(functools.partial(body, member))

    def send_pieces(*steps):
        def body(member):
            for k in steps:
                for item, condition, copy in sends(member, k):
                    if item is not None:
                        wait_for(member, item)
                    when(condition, copy.start)

        on_each(body)

    def table_copy(n, source, target, peer):
        return pltpu.make_async_remote_copy(
            src_ref=source, dst_ref=target, send_sem=table_send_sem.at[n], recv_sem=table_recv_sem.at[n],
            device_id=peer, device_id_type=MESH,
        )

    load = pltpu.make_async_copy(fields_ref, held, local_sem)
    load.start()
    send_pieces(0)

    lane = lax.broadcasted_iota(jnp.int32, (1, table_ref.shape[1]), 1)
    taken = jnp.zeros(lane.shape, jnp.float32)
    for row in range(rows):
        departure = departure_of(row, first_row, rows, total_rows, departure_ref, extents_ref)
        lon_w = cubic(lon_t_ref[row])
        share = area_ref[first_row + row] * (lon_w[0] + lon_w[1] + lon_w[2] + lon_w[3]) * (1.0 / levs)
        for a, weight in enumerate(cubic(lat_t_ref[row])):
            taken = taken + jnp.where(lane == departure - 1 + a, share * weight, 0.0)
    load.wait()
    sums = [jnp.zeros(lane.shape, jnp.float32) for _ in range(field_count)]
    for row in range(rows):
        for f in range(field_count):
            total = jnp.sum(jnp.sum(held[row, f], axis=0, keepdims=True), axis=1, keepdims=True)
            sums[f] = sums[f] + jnp.where(lane == first_row + row, total, 0.0)
    mine[...] = jnp.zeros_like(mine)
    for f in range(field_count):
        mine[f:f + 1, :] = sums[f]
    mine[field_count:field_count + 1, :] = taken

    def table_step(n):
        return table_copy(n, mine if n == 0 else sent.at[n - 1], met.at[n], across[n])

    def table_add(n):
        table_step(n).wait_recv()
        sent[n] = (mine[...] if n == 0 else sent[n - 1]) + met[n]

    table_step(0).start()
    table_add(0)
    table_step(1).start()
    send_pieces(1, 2)
    table_add(1)
    table_step(2).start()
    send_pieces(3, 4)
    table_add(2)
    last = [table_copy(3 + j, sent.at[2], gathered.at[j], peer) for j, peer in enumerate(others)]
    for copy in last:
        copy.start()
    send_pieces(5, 6)
    for copy in last:
        copy.wait_recv()
    result = sent[2]
    for j in range(len(others)):
        result = result + gathered[j]
    table_ref[...] = result

    def finish(member):
        for k in range(7):
            for link in LINKS:
                items = arrivals(member)[link]
                if k < len(items):
                    wait_for(member, items[k])
        for k in range(7):
            for _, condition, copy in sends(member, k):
                when(condition, copy.wait_send)

    on_each(finish)
    for n in range(3):
        table_step(n).wait_send()
    for copy in last:
        copy.wait_send()


def exchange(lat_t, lon_t, departure_row, extents, area, fields):
    bands, levs = lax.axis_size("lat"), lax.axis_size("lev")
    rows, field_count = fields.shape[:2]
    table = ((field_count + 8) // 8 * 8, -(-bands * rows // LANES) * LANES)
    others = bands // 4 - 1
    return pl.pallas_call(
        functools.partial(exchange_kernel, bands, levs),
        out_shape=(
            jax.ShapeDtypeStruct((2 * REACH * rows,) + fields.shape[1:], fields.dtype),
            jax.ShapeDtypeStruct(table, jnp.float32),
        ),
        in_specs=[pl.BlockSpec(memory_space=pltpu.SMEM)] * 5 + [pl.BlockSpec(memory_space=pl.ANY)],
        out_specs=(pl.BlockSpec(memory_space=pl.ANY), pl.BlockSpec(memory_space=pltpu.VMEM)),
        scratch_shapes=[
            pltpu.VMEM(fields.shape, jnp.float32),
            pltpu.VMEM(table, jnp.float32),
            pltpu.VMEM((3,) + table, jnp.float32),
            pltpu.VMEM((3,) + table, jnp.float32),
            pltpu.VMEM((max(others, 1),) + table, jnp.float32),
            pltpu.SemaphoreType.DMA((4, 7)),
            pltpu.SemaphoreType.DMA((4, 7)),
            pltpu.SemaphoreType.DMA,
            pltpu.SemaphoreType.DMA((3 + others,)),
            pltpu.SemaphoreType.DMA((3 + others,)),
        ],
        compiler_params=pltpu.CompilerParams(collective_id=0, has_side_effects=True),
        name="exchange",
    )(lat_t, lon_t, departure_row, extents, area, fields)


def row_kernel(bands, lat_t_ref, lon_t_ref, shift_ref, departure_ref, extents_ref, table_ref, area_ref, fields_ref,
               halo_ref, out_ref, held, doubled, ratio, sem):
    row = pl.program_id(0)
    row_count = pl.num_programs(0)
    rows, field_count, _, lon_count = fields_ref.shape
    tiles = lon_count // LANES
    depth = held.shape[0]
    first_row = lax.axis_index("lat") * rows

    def fetch(index):
        slot = lax.rem(index, depth)
        departure = departure_of(index, first_row, rows, bands * rows, departure_ref, extents_ref)
        start = departure - 1 - (first_row - REACH * rows)
        low, high = REACH * rows, (REACH + 1) * rows
        outside = jnp.logical_or(start + 4 <= low, start >= high)

        @pl.when(outside)
        def _():
            away = jnp.where(start < low, start, start - rows)
            pltpu.make_async_copy(halo_ref.at[pl.ds(away, 4)], held.at[slot], sem.at[slot]).start()

        @pl.when(jnp.logical_not(outside))
        def _():
            for a in range(4):
                place = start + a
                own = jnp.logical_and(place >= low, place < high)
                target = held.at[slot, a]

                @pl.when(own)
                def _():
                    pltpu.make_async_copy(fields_ref.at[place - low], target, sem.at[slot]).start()

                @pl.when(jnp.logical_not(own))
                def _():
                    away = jnp.where(place < low, place, place - rows)
                    pltpu.make_async_copy(halo_ref.at[away], target, sem.at[slot]).start()

    @pl.when(row == 0)
    def _():
        for index in range(min(depth - 1, rows)):
            fetch(index)
        weight = table_ref[field_count:field_count + 1, :]
        for f in range(field_count):
            total = table_ref[f:f + 1, :]
            before = jnp.sum(total * area_ref[...], axis=1, keepdims=True)
            after = jnp.sum(total * weight, axis=1, keepdims=True)
            ratio[f] = jnp.broadcast_to(before / after, ratio.shape[1:])

    @pl.when(row + depth - 1 < row_count)
    def _():
        fetch(row + depth - 1)

    slot = lax.rem(row, depth)
    pltpu.make_async_copy(halo_ref.at[pl.ds(0, 4)], held.at[slot], sem.at[slot]).wait()
    lat_w, lon_w = cubic(lat_t_ref[row]), cubic(lon_t_ref[row])
    lane = lax.broadcasted_iota(jnp.int32, (out_ref.shape[2], LANES), 1)
    first = lax.rem(shift_ref[row] - 1 + lon_count, lon_count)
    whole, rest = first // LANES, lax.rem(first, LANES)
    turn = lax.rem(LANES - rest, LANES)
    keep = lane < LANES - rest

    def ahead(pieces, step):
        turned = [pltpu.roll(piece, LANES - step, 1) for piece in pieces]
        return [jnp.where(lane < LANES - step, turned[t], turned[(t + 1) % tiles]) for t in range(tiles)]

    for f in range(field_count):
        lon = [weight * ratio[f] for weight in lon_w]
        column = []
        for t in range(tiles):
            at = pl.ds(t * LANES, LANES)
            total = lat_w[0] * held[slot, 0, f, :, at]
            for a in range(1, 4):
                total = total + lat_w[a] * held[slot, a, f, :, at]
            column.append(total)
        after = ahead(column, 1)
        later = ahead([lon[2] * column[t] + lon[3] * after[t] for t in range(tiles)], 2)
        for t in range(tiles):
            mixed = lon[0] * column[t] + lon[1] * after[t] + later[t]
            doubled[f, :, t * LANES:(t + 1) * LANES] = mixed
            doubled[f, :, lon_count + t * LANES:lon_count + (t + 1) * LANES] = mixed
        turned = []
        for t in range(tiles + 1):
            at = pl.multiple_of((whole + t) * LANES, LANES)
            turned.append(pltpu.roll(doubled[f, :, pl.ds(at, LANES)], turn, 1))
        for t in range(tiles):
            out_ref[0, f, :, t * LANES:(t + 1) * LANES] = jnp.where(keep, turned[t], turned[t + 1])


def rows_of(bands, lat_t, lon_t, shift, departure_row, extents, table, area, fields, halo):
    rows, field_count, levels, lon_count = fields.shape
    smem = pl.BlockSpec(memory_space=pltpu.SMEM)
    return pl.pallas_call(
        functools.partial(row_kernel, bands),
        grid=(rows,),
        out_shape=jax.ShapeDtypeStruct(fields.shape, fields.dtype),
        in_specs=[smem] * 5 + [pl.BlockSpec(memory_space=pltpu.VMEM)] * 2 + [pl.BlockSpec(memory_space=pl.ANY)] * 2,
        out_specs=pl.BlockSpec((1, field_count, levels, lon_count), lambda r: (r, 0, 0, 0)),
        scratch_shapes=[
            pltpu.VMEM((DEPTH, 4, field_count, levels, lon_count), jnp.float32),
            pltpu.VMEM((field_count, levels, 2 * lon_count), jnp.float32),
            pltpu.VMEM((field_count, levels, LANES), jnp.float32),
            pltpu.SemaphoreType.DMA((DEPTH,)),
        ],
        compiler_params=pltpu.CompilerParams(dimension_semantics=("arbitrary",)),
        name="rows",
    )(lat_t, lon_t, shift, departure_row, extents, table, area, fields, halo)


def per_device(fields, lat_fraction, lon_fraction, lon_shift, departure_row, extents):
    bands = lax.axis_size("lat")
    total_rows = bands * fields.shape[0]
    row_ids = np.arange(-(-total_rows // LANES) * LANES)
    area = np.where(row_ids < total_rows, np.cos(math.pi * (row_ids + 0.5) / total_rows - math.pi / 2.0), 0.0)
    area = jnp.asarray(area, jnp.float32)
    halo, table = exchange(lat_fraction, lon_fraction, departure_row, extents, area, fields)
    return rows_of(
        bands, lat_fraction, lon_fraction, lon_shift, departure_row, extents, table, area[None, :], fields, halo
    )


def solution(mesh):
    return jax.shard_map(
        per_device,
        mesh=mesh,
        in_specs=(
            P("lat", None, "lev", None),
            P("lat"),
            P("lat"),
            P("lat"),
            P("lat"),
            P("lat", None),
        ),
        out_specs=P("lat", None, "lev", None),
        check_vma=False,
    )
```

profile of v0, /device:TPU:0, one launch (start us, length us, event | category | flops | bytes accessed | tf_op | source)
XLA Modules:
  0.0 138.6 jit_solution(7545594031537522428)
XLA Ops:
  0.0 130.8 %exchange.1 = (f32[80,3,8,2560]{3,2,1,0:T(8,128)}, f32[8,256]{1,0:T(8,128)}) custom-call(f32[10]{0:T(128)} %lat_t_ref.3, f32[10]{0:T(128)} %lon_t_ref.3, s32[10]{0:T(128)} %departure_ref.3, s32[1,2]{1,0:T(1,128)} %extents_ref.3, f32[256]{0:T(256)} %constant.2.clone.area_ref, f32[10,3,8,2560]{3,2,1,0:T(8,128)} %fields_ref.3), custom_call_target="tpu_custom_call" | custom-call | tf_op jit(solution)/shard_map/exchange/pallas_call | solution.py:232
  130.8 7.8 %rows.1 = f32[10,3,8,2560]{3,2,1,0:T(8,128)} custom-call(f32[10]{0:T(128)} %lat_t_ref.3, f32[10]{0:T(128)} %lon_t_ref.3, s32[10]{0:T(128)} %shift_ref.1, s32[10]{0:T(128)} %departure_ref.3, s32[1,2]{1,0:T(1,128)} %extents_ref.3, f32[8,256]{1,0:T(8,128)} %get-tuple-element.7.table_ref, f32[1,256]{1,0:T(1,128)} %constant.9.area_ref, ...), custom_call_target="tpu_custom_call" | custom-call | tf_op jit(solution)/shard_map/rows/pallas_call | solution.py:348
where the time goes:
time: 139 us
  Pallas kernels  139 us (100%)
    pallas_call x1, Pallas kernels, exchange(): pl.pallas_call(functools.partial(exchange_kernel, bands, levs), out_shape...  131 us
    pallas_call x1, Pallas kernels, rows_of(): pl.pallas_call(functools.partial(row_kernel, bands), grid=(rows,), out_sh...  7.84 us

commit v1 on v0

v1 whole, which is shorter than its diff:
```python
import functools
import math

import jax
import jax.numpy as jnp
import numpy as np
from jax import lax
from jax.experimental import pallas as pl
from jax.experimental.pallas import tpu as pltpu
from jax.sharding import PartitionSpec as P

GROUP = 4
LANES = 128
PARTS = 5
LEAD = 4
LAG = 2
MESH = pl.DeviceIdType.MESH


def cubic(t):
    sixth = 1.0 / 6.0
    return (
        -t * (t - 1.0) * (t - 2.0) * sixth,
        (t + 1.0) * (t - 1.0) * (t - 2.0) * 0.5,
        -(t + 1.0) * t * (t - 2.0) * 0.5,
        (t + 1.0) * t * (t - 1.0) * sixth,
    )


def departure_of(departure, north, south, first_row, rows, total_rows):
    low = first_row - north * rows + 1
    high = first_row + rows - 3 + south * rows
    inside = jnp.minimum(jnp.maximum(departure, low), high)
    return jnp.minimum(jnp.maximum(inside, 1), total_rows - 3)


def chunks_of(field_count, lon_count):
    tiles = lon_count // (GROUP * LANES)
    parts = min(PARTS, tiles)
    edges = [tiles * n // parts for n in range(parts + 1)]
    return [
        (f, edges[n] * LANES, (edges[n + 1] - edges[n]) * LANES) for f in range(field_count) for n in range(parts)
    ]


def exchange_kernel(bands, levs, chunks, lat_t_ref, lon_t_ref, departure_ref, extents_ref, area_ref, fields_ref,
                    column_ref, table_ref, held, far_departure, far_extents, far_lat, start_of, weight_of, mine, met,
                    sent, gathered, load_sem, note_send, note_recv, give_send, give_recv, pass_send, pass_recv,
                    slice_sem, bring_send, bring_recv, keep_sem, table_send_sem, table_recv_sem, *buffers):
    band, lev = lax.axis_index("lat"), lax.axis_index("lev")
    group, position = band // GROUP, lax.rem(band, GROUP)
    groups = bands // GROUP
    has_up = group < groups - 1
    has_down = group > 0
    rows, field_count, _, lon_count = fields_ref.shape
    width = lon_count // GROUP
    count = len(chunks)
    source, mixed = buffers[:count], buffers[count:]
    first_row, total_rows = band * rows, bands * rows
    step_one = 1 - 2 * lax.rem(position, 2)
    step_two = 2 - 4 * (position // 2)
    steps = [step_one, step_two, step_one + step_two]
    across = [{"lev": 1 - lev}, {"lat": band + step_one}, {"lat": band + step_two}]
    others = [{"lat": lax.rem(band + GROUP * j, bands)} for j in range(1, groups)]

    load = pltpu.make_async_copy(fields_ref, held, load_sem)
    load.start()

    barrier = pltpu.get_barrier_semaphore()
    greeted = across + [{"lat": band + steps[2]}] + others
    for peer in greeted:
        pl.semaphore_signal(barrier, inc=1, device_id=peer, device_id_type=MESH)
    pl.semaphore_wait(barrier, len(greeted))

    def remote(source_ref, target_ref, send_sem, recv_sem, peer):
        return pltpu.make_async_remote_copy(
            src_ref=source_ref, dst_ref=target_ref, send_sem=send_sem, recv_sem=recv_sem,
            device_id=peer, device_id_type=MESH,
        )

    def slice_at(home, k):
        first, size = chunks[k][1:]
        return pl.ds(pl.multiple_of(home * width + first, LANES), size)

    def fields_cut(home, k):
        return fields_ref.at[:, chunks[k][0], :, slice_at(home, k)]

    def source_cut(k, n):
        return source[k].at[pl.ds(n * rows, rows)]

    def note(n, j):
        here, there = ((departure_ref, far_departure), (extents_ref.at[0], far_extents), (lat_t_ref, far_lat))[n]
        return remote(here, there.at[position], note_send.at[n, j], note_recv.at[n, j], {"lat": band + steps[j]})

    def give(j, k):
        home = position + steps[j]
        return remote(
            fields_cut(home, k), source_cut(k, GROUP + position), give_send.at[j], give_recv.at[j, k],
            {"lat": band + steps[j]},
        )

    def own_slice(k):
        return pltpu.make_async_copy(fields_cut(position, k), source_cut(k, GROUP + position), slice_sem.at[k])

    def pass_on(k, member, block):
        up = remote(
            block, source_cut(k, member), pass_send.at[0], pass_recv.at[0, k], {"lat": band + GROUP}
        )
        down = remote(
            block, source_cut(k, 2 * GROUP + member), pass_send.at[1], pass_recv.at[1, k], {"lat": band - GROUP}
        )
        pl.when(has_up)(up.start)
        pl.when(has_down)(down.start)

    def bring(j, k):
        return remote(
            mixed[k].at[pl.ds((position + steps[j]) * rows, rows)],
            column_ref.at[:, chunks[k][0], :, slice_at(position, k)],
            bring_send.at[j], bring_recv.at[j, k], {"lat": band + steps[j]},
        )

    def keep(k):
        return pltpu.make_async_copy(
            mixed[k].at[pl.ds(position * rows, rows)],
            column_ref.at[:, chunks[k][0], :, slice_at(position, k)], keep_sem.at[k],
        )

    def table_copy(n, block, target, peer):
        return remote(block, target, table_send_sem.at[n], table_recv_sem.at[n], peer)

    def table_step(n):
        return table_copy(n, mine if n == 0 else sent.at[n - 1], met.at[n], across[n])

    def table_add(n):
        table_step(n).wait_recv()
        sent[n] = (mine[...] if n == 0 else sent[n - 1]) + met[n]

    last = [table_copy(3 + j, sent.at[2], gathered.at[j], peer) for j, peer in enumerate(others)]

    def pass_own(k):
        if k < count:
            pass_on(k, position, fields_cut(position, k))

    def take(k):
        for j in range(3):
            give(j, k).wait_recv()
            member = position + steps[j]
            pass_on(k, member, source_cut(k, GROUP + member))
        pass_own(k + LEAD)

    def combine(k):
        own_slice(k).wait()

        @pl.when(has_down)
        def _():
            block = source[k].at[pl.ds(0, GROUP * rows)]
            remote(block, block, pass_send.at[0], pass_recv.at[0, k], {"lat": band}).wait_recv()

        @pl.when(has_up)
        def _():
            block = source[k].at[pl.ds(2 * GROUP * rows, GROUP * rows)]
            remote(block, block, pass_send.at[1], pass_recv.at[1, k], {"lat": band}).wait_recv()

        def one_row(n, carry):
            first = start_of[n]
            weights = [weight_of[GROUP * n + a] for a in range(4)]
            for t in range(chunks[k][2] // LANES):
                at = pl.ds(t * LANES, LANES)
                total = weights[0] * source[k][first, :, at]
                for a in range(1, 4):
                    total = total + weights[a] * source[k][first + a, :, at]
                mixed[k][n, :, at] = total
            return carry

        lax.fori_loop(0, GROUP * rows, one_row, 0, unroll=4)
        for j in range(3):
            bring(j, k).start()
        keep(k).start()

    for n in range(3):
        for j in range(3):
            note(n, j).start()
    for k in range(count):
        for j in range(3):
            give(j, k).start()
        if k < LEAD:
            pass_own(k)
    for k in range(count):
        own_slice(k).start()

    lane = lax.broadcasted_iota(jnp.int32, (1, table_ref.shape[1]), 1)
    taken = jnp.zeros(lane.shape, jnp.float32)
    for row in range(rows):
        departure = departure_of(
            departure_ref[row], extents_ref[0, 0], extents_ref[0, 1], first_row, rows, total_rows
        )
        lon_w = cubic(lon_t_ref[row])
        share = area_ref[first_row + row] * (lon_w[0] + lon_w[1] + lon_w[2] + lon_w[3]) * (1.0 / levs)
        for a, weight in enumerate(cubic(lat_t_ref[row])):
            taken = taken + jnp.where(lane == departure - 1 + a, share * weight, 0.0)
    load.wait()
    sums = [jnp.zeros(lane.shape, jnp.float32) for _ in range(field_count)]
    for row in range(rows):
        for f in range(field_count):
            total = jnp.sum(jnp.sum(held[row, f], axis=0, keepdims=True), axis=1, keepdims=True)
            sums[f] = sums[f] + jnp.where(lane == first_row + row, total, 0.0)
    mine[...] = jnp.zeros_like(mine)
    for f in range(field_count):
        mine[f:f + 1, :] = sums[f]
    mine[field_count:field_count + 1, :] = taken
    table_step(0).start()

    take(0)
    for row in range(rows):
        far_departure[position, row] = departure_ref[row]
        far_lat[position, row] = lat_t_ref[row]
    for e in range(2):
        far_extents[position, e] = extents_ref[0, e]
    for n in range(3):
        for j in range(3):
            note(n, j).wait_recv()
    for member in range(GROUP):
        member_row = (group * GROUP + member) * rows
        north, south = far_extents[member, 0], far_extents[member, 1]

        def prepare(row, carry):
            departure = departure_of(far_departure[member, row], north, south, member_row, rows, total_rows)
            start_of[member * rows + row] = departure - 1 - (group - 1) * GROUP * rows
            for a, weight in enumerate(cubic(far_lat[member, row])):
                weight_of[GROUP * (member * rows + row) + a] = weight
            return carry

        lax.fori_loop(0, rows, prepare, 0)

    table_add(0)
    table_step(1).start()
    done = 0
    for k in range(1, count):
        take(k)
        while done < count and 2 * done + 1 + LAG <= k:
            combine(done)
            done += 1
        if k == count // 3:
            table_add(1)
            table_step(2).start()
        if k == count - 1:
            table_add(2)
            for copy in last:
                copy.start()
    while done < count:
        combine(done)
        done += 1

    for copy in last:
        copy.wait_recv()
    result = sent[2]
    for j in range(len(others)):
        result = result + gathered[j]
    table_ref[...] = result

    for k in range(count):
        for j in range(3):
            home = position + steps[j]
            block = column_ref.at[:, chunks[k][0], :, slice_at(home, k)]
            remote(block, block, bring_send.at[j], bring_recv.at[j, k], {"lat": band}).wait_recv()
        keep(k).wait()
    for k in range(count):
        for j in range(3):
            give(j, k).wait_send()
            bring(j, k).wait_send()
        for _ in range(GROUP):
            @pl.when(has_up)
            def _():
                remote(
                    source_cut(k, 0), source_cut(k, 0), pass_send.at[0], pass_recv.at[0, k], {"lat": band}
                ).wait_send()

            @pl.when(has_down)
            def _():
                remote(
                    source_cut(k, 0), source_cut(k, 0), pass_send.at[1], pass_recv.at[1, k], {"lat": band}
                ).wait_send()
    for n in range(3):
        for j in range(3):
            note(n, j).wait_send()
        table_step(n).wait_send()
    for copy in last:
        copy.wait_send()


def exchange(lat_t, lon_t, departure_row, extents, area, fields):
    bands, levs = lax.axis_size("lat"), lax.axis_size("lev")
    rows, field_count, levels, lon_count = fields.shape
    table = ((field_count + 8) // 8 * 8, -(-bands * rows // LANES) * LANES)
    others = bands // GROUP - 1
    chunks = chunks_of(field_count, lon_count)
    count = len(chunks)
    dma = pltpu.SemaphoreType.DMA
    return pl.pallas_call(
        functools.partial(exchange_kernel, bands, levs, chunks),
        out_shape=(
            jax.ShapeDtypeStruct(fields.shape, fields.dtype),
            jax.ShapeDtypeStruct(table, jnp.float32),
        ),
        in_specs=[pl.BlockSpec(memory_space=pltpu.SMEM)] * 5 + [pl.BlockSpec(memory_space=pl.ANY)],
        out_specs=(pl.BlockSpec(memory_space=pl.ANY), pl.BlockSpec(memory_space=pltpu.VMEM)),
        scratch_shapes=[
            pltpu.VMEM(fields.shape, jnp.float32),
            pltpu.SMEM((GROUP, rows), jnp.int32),
            pltpu.SMEM((GROUP, 2), jnp.int32),
            pltpu.SMEM((GROUP, rows), jnp.float32),
            pltpu.SMEM((GROUP * rows,), jnp.int32),
            pltpu.SMEM((4 * GROUP * rows,), jnp.float32),
            pltpu.VMEM(table, jnp.float32),
            pltpu.VMEM((3,) + table, jnp.float32),
            pltpu.VMEM((3,) + table, jnp.float32),
            pltpu.VMEM((max(others, 1),) + table, jnp.float32),
            dma,
            dma((3, 3)),
            dma((3, 3)),
            dma((3,)),
            dma((3, count)),
            dma((2,)),
            dma((2, count)),
            dma((count,)),
            dma((3,)),
            dma((3, count)),
            dma((count,)),
            dma((3 + others,)),
            dma((3 + others,)),
        ]
        + [pltpu.VMEM((3 * GROUP * rows, levels, size), jnp.float32) for _, _, size in chunks]
        + [pltpu.VMEM((GROUP * rows, levels, size), jnp.float32) for _, _, size in chunks],
        compiler_params=pltpu.CompilerParams(collective_id=0, has_side_effects=True),
        name="exchange",
    )(lat_t, lon_t, departure_row, extents, area, fields)


def row_kernel(lon_t_ref, shift_ref, table_ref, area_ref, column_ref, out_ref, doubled, ratio):
    row = pl.program_id(0)
    _, field_count, _, lon_count = column_ref.shape
    tiles = lon_count // LANES

    @pl.when(row == 0)
    def _():
        weight = table_ref[field_count:field_count + 1, :]
        for f in range(field_count):
            total = table_ref[f:f + 1, :]
            before = jnp.sum(total * area_ref[...], axis=1, keepdims=True)
            after = jnp.sum(total * weight, axis=1, keepdims=True)
            ratio[f] = jnp.broadcast_to(before / after, ratio.shape[1:])

    lon_w = cubic(lon_t_ref[row])
    lane = lax.broadcasted_iota(jnp.int32, (out_ref.shape[2], LANES), 1)
    first = lax.rem(shift_ref[row] - 1 + lon_count, lon_count)
    whole, rest = first // LANES, lax.rem(first, LANES)
    turn = lax.rem(LANES - rest, LANES)
    keep = lane < LANES - rest

    def ahead(pieces, step):
        turned = [pltpu.roll(piece, LANES - step, 1) for piece in pieces]
        return [jnp.where(lane < LANES - step, turned[t], turned[(t + 1) % tiles]) for t in range(tiles)]

    for f in range(field_count):
        lon = [weight * ratio[f] for weight in lon_w]
        column = [column_ref[0, f, :, t * LANES:(t + 1) * LANES] for t in range(tiles)]
        after = ahead(column, 1)
        later = ahead([lon[2] * column[t] + lon[3] * after[t] for t in range(tiles)], 2)
        for t in range(tiles):
            moved = lon[0] * column[t] + lon[1] * after[t] + later[t]
            doubled[f, :, t * LANES:(t + 1) * LANES] = moved
            doubled[f, :, lon_count + t * LANES:lon_count + (t + 1) * LANES] = moved
        turned = []
        for t in range(tiles + 1):
            at = pl.multiple_of((whole + t) * LANES, LANES)
            turned.append(pltpu.roll(doubled[f, :, pl.ds(at, LANES)], turn, 1))
        for t in range(tiles):
            out_ref[0, f, :, t * LANES:(t + 1) * LANES] = jnp.where(keep, turned[t], turned[t + 1])


def rows_of(lon_t, shift, table, area, column):
    rows, field_count, levels, lon_count = column.shape
    smem = pl.BlockSpec(memory_space=pltpu.SMEM)
    vmem = pl.BlockSpec(memory_space=pltpu.VMEM)
    row_block = pl.BlockSpec((1, field_count, levels, lon_count), lambda r: (r, 0, 0, 0))
    return pl.pallas_call(
        row_kernel,
        grid=(rows,),
        out_shape=jax.ShapeDtypeStruct(column.shape, column.dtype),
        in_specs=[smem, smem, vmem, vmem, row_block],
        out_specs=row_block,
        scratch_shapes=[
            pltpu.VMEM((field_count, levels, 2 * lon_count), jnp.float32),
            pltpu.VMEM((field_count, levels, LANES), jnp.float32),
        ],
        compiler_params=pltpu.CompilerParams(dimension_semantics=("arbitrary",)),
        name="rows",
    )(lon_t, shift, table, area, column)


def per_device(fields, lat_fraction, lon_fraction, lon_shift, departure_row, extents):
    bands = lax.axis_size("lat")
    total_rows = bands * fields.shape[0]
    row_ids = np.arange(-(-total_rows // LANES) * LANES)
    area = np.where(row_ids < total_rows, np.cos(math.pi * (row_ids + 0.5) / total_rows - math.pi / 2.0), 0.0)
    area = jnp.asarray(area, jnp.float32)
    column, table = exchange(lat_fraction, lon_fraction, departure_row, extents, area, fields)
    return rows_of(lon_fraction, lon_shift, table, area[None, :], column)


def solution(mesh):
    return jax.shard_map(
        per_device,
        mesh=mesh,
        in_specs=(
            P("lat", None, "lev", None),
            P("lat"),
            P("lat"),
            P("lat"),
            P("lat"),
            P("lat", None),
        ),
        out_specs=P("lat", None, "lev", None),
        check_vma=False,
    )
```

time: 139 us -> 79 us (0.57)
  Pallas kernels: 139 us -> 78.7 us
    pallas_call x2, Pallas kernels: 139 us -> 78.7 us  [the longest x1 70.1 us: exchange(): pl.pallas_call(functools.partial(exchange_kernel, bands, levs, chunks), o...]
where the time goes in v1:
time: 79 us; the launch traced here: 78.7 us
  Pallas kernels  78.7 us (100%)
    pallas_call x1, Pallas kernels, exchange(): pl.pallas_call(functools.partial(exchange_kernel, bands, levs, chunks), o...  70.1 us
    pallas_call x1, Pallas kernels, rows_of(): pl.pallas_call(row_kernel, grid=(rows,), out_shape=jax.ShapeDtypeStruct(c...  8.53 us

profile of v1, /device:TPU:0, one launch (start us, length us, event | category | flops | bytes accessed | tf_op | source)
XLA Modules:
  0.0 78.7 jit_solution(9326691111496789764)
XLA Ops:
  0.0 70.1 %exchange.1 = (f32[10,3,8,2560]{3,2,1,0:T(8,128)}, f32[8,256]{1,0:T(8,128)}) custom-call(f32[10]{0:T(128)} %lat_t_ref.1, f32[10]{0:T(128)} %lon_t_ref.3, s32[10]{0:T(128)} %departure_ref.1, s32[1,2]{1,0:T(1,128)} %extents_ref.1, f32[256]{0:T(256)} %constant.2.clone.area_ref, f32[10,3,8,2560]{3,2,1,0:T(8,128)} %fields_ref.1), custom_call_target="tpu_custom_call" | custom-call | tf_op jit(solution)/shard_map/exchange/pallas_call | solution.py:299
  70.1 8.5 %rows.1 = f32[10,3,8,2560]{3,2,1,0:T(8,128)} custom-call(f32[10]{0:T(128)} %lon_t_ref.3, s32[10]{0:T(128)} %shift_ref.1, f32[8,256]{1,0:T(8,128)} %get-tuple-element.7.table_ref, f32[1,256]{1,0:T(1,128)} %constant.9.area_ref, f32[10,3,8,2560]{3,2,1,0:T(8,128)} %get-tuple-element.8.column_ref), custom_call_target="tpu_custom_call" | custom-call | tf_op jit(solution)/shard_map/rows/pallas_call | solution.py:386

commit v2 on v1

v2 whole, which is shorter than its diff:
```python
import functools
import math

import jax
import jax.numpy as jnp
import numpy as np
from jax import lax
from jax.experimental import pallas as pl
from jax.experimental.pallas import tpu as pltpu
from jax.sharding import PartitionSpec as P

GROUP = 4
LANES = 128
PARTS = (3, 3, 3)
GIVEN = 4
PASSED = 2
WAIT = 1
VMEM_BYTES = 40 * 1024 * 1024
MESH = pl.DeviceIdType.MESH


def cubic(t):
    sixth = 1.0 / 6.0
    return (
        -t * (t - 1.0) * (t - 2.0) * sixth,
        (t + 1.0) * (t - 1.0) * (t - 2.0) * 0.5,
        -(t + 1.0) * t * (t - 2.0) * 0.5,
        (t + 1.0) * t * (t - 1.0) * sixth,
    )


def departure_of(departure, north, south, first_row, rows, total_rows):
    low = first_row - north * rows + 1
    high = first_row + rows - 3 + south * rows
    inside = jnp.minimum(jnp.maximum(departure, low), high)
    return jnp.minimum(jnp.maximum(inside, 1), total_rows - 3)


def chunks_of(field_count, lon_count):
    tiles = lon_count // (GROUP * LANES)
    chunks = []
    for f in range(field_count):
        parts = min(PARTS[min(f, len(PARTS) - 1)], tiles)
        edges = [tiles * n // parts for n in range(parts + 1)]
        if f == field_count - 1:
            edges = [tiles - edge for edge in reversed(edges)]
        chunks += [(f, low * LANES, (high - low) * LANES) for low, high in zip(edges, edges[1:])]
    return chunks


def advect_kernel(bands, levs, chunks, lat_t_hbm, lon_t_hbm, shift_hbm, departure_hbm, extents_hbm, area_hbm,
                  fields_ref, moved_ref, lat_t_ref, lon_t_ref, shift_ref, departure_ref, extents_ref,
                  area_ref, held, far_departure, far_extents, far_lat, start_of, weight_of, lon_of, mine, met, plane,
                  below, above, upward, downward, ratio, scalar_sem, load_sem, note_send, note_recv, give_send,
                  give_recv, pass_send, pass_recv, slice_sem, bring_send, bring_recv, keep_sem, table_send,
                  table_recv, chain_send, chain_recv, *buffers):
    band, lev = lax.axis_index("lat"), lax.axis_index("lev")
    group, position = band // GROUP, lax.rem(band, GROUP)
    groups = bands // GROUP
    has_up = group < groups - 1
    has_down = group > 0
    rows, field_count, levels, lon_count = fields_ref.shape
    width = lon_count // GROUP
    tiles = lon_count // LANES
    count = len(chunks)
    source, mixed = buffers[:count], buffers[count:2 * count]
    column = buffers[2 * count:]
    first_row, total_rows = band * rows, bands * rows
    step_one = 1 - 2 * lax.rem(position, 2)
    step_two = 2 - 4 * (position // 2)
    steps = [step_one, step_two, step_one + step_two]
    mates = [{"lat": band + step, "lev": (lev + n) % levs} for n in range(levs) for step in [0] + steps][1:]
    up_peer, down_peer = {"lat": band + GROUP}, {"lat": band - GROUP}

    def signal(peer):
        pl.semaphore_signal(barrier, inc=1, device_id=peer, device_id_type=MESH)

    barrier = pltpu.get_barrier_semaphore()
    for peer in mates:
        signal(peer)
    pl.when(has_up)(lambda: signal(up_peer))
    pl.when(has_down)(lambda: signal(down_peer))

    scalars = [
        pltpu.make_async_copy(there, here, scalar_sem.at[n])
        for n, (there, here) in enumerate((
            (departure_hbm, departure_ref), (extents_hbm, extents_ref), (lat_t_hbm, lat_t_ref),
            (lon_t_hbm, lon_t_ref), (shift_hbm, shift_ref), (area_hbm, area_ref),
        ))
    ]
    for copy in scalars:
        copy.start()
    load = pltpu.make_async_copy(fields_ref, held, load_sem)
    load.start()

    pl.semaphore_wait(barrier, len(mates) + has_up.astype(jnp.int32) + has_down.astype(jnp.int32))

    def remote(source_ref, target_ref, send_sem, recv_sem, peer):
        return pltpu.make_async_remote_copy(
            src_ref=source_ref, dst_ref=target_ref, send_sem=send_sem, recv_sem=recv_sem,
            device_id=peer, device_id_type=MESH,
        )

    def slice_at(home, k):
        first, size = chunks[k][1:]
        return pl.ds(pl.multiple_of(home * width + first, LANES), size)

    def fields_cut(home, k):
        return fields_ref.at[:, chunks[k][0], :, slice_at(home, k)]

    def source_cut(k, n, blocks=1):
        return source[k].at[pl.ds(n * rows, blocks * rows)]

    def column_cut(home, k):
        f, first, size = chunks[k]
        return column[f].at[:, pl.ds((home * width + first) // LANES, size // LANES)]

    def note(n, j):
        here, there = ((departure_ref, far_departure), (extents_ref.at[0], far_extents), (lat_t_ref, far_lat))[n]
        return remote(here, there.at[position], note_send.at[n, j], note_recv.at[n, j], {"lat": band + steps[j]})

    def give(j, k):
        home = position + steps[j]
        return remote(
            fields_cut(home, k), source_cut(k, GROUP + position), give_send.at[j], give_recv.at[j, k],
            {"lat": band + steps[j]},
        )

    def own_slice(k):
        return pltpu.make_async_copy(fields_cut(position, k), source_cut(k, GROUP + position), slice_sem.at[k])

    def pass_up(k, block, n, blocks=1):
        return remote(block, source_cut(k, n, blocks), pass_send.at[0], pass_recv.at[0, k], up_peer)

    def pass_down(k, block, n, blocks=1):
        return remote(block, source_cut(k, 2 * GROUP + n, blocks), pass_send.at[1], pass_recv.at[1, k], down_peer)

    def pass_on(k, member, block):
        pl.when(has_up)(pass_up(k, block, member).start)
        pl.when(has_down)(pass_down(k, block, member).start)

    def bring(j, k):
        return remote(
            mixed[k].at[pl.ds((position + steps[j]) * rows, rows)], column_cut(position, k),
            bring_send.at[j], bring_recv.at[j, k], {"lat": band + steps[j]},
        )

    def keep(k):
        return pltpu.make_async_copy(
            mixed[k].at[pl.ds(position * rows, rows)], column_cut(position, k), keep_sem.at[k]
        )

    def table_copy(n):
        return remote(mine, met.at[n], table_send.at[n], table_recv.at[n], mates[n])

    up_copy = remote(upward, below, chain_send.at[0], chain_recv.at[0], up_peer)
    down_copy = remote(downward, above, chain_send.at[1], chain_recv.at[1], down_peer)

    def give_all(k):
        if k < count:
            for j in range(3):
                give(j, k).start()

    def pass_own(k):
        if k < count:
            pass_on(k, position, fields_cut(position, k))

    def take(k):
        if k >= count:
            return
        for j in range(3):
            give(j, k).wait_recv()
            member = position + steps[j]
            pass_on(k, member, source_cut(k, GROUP + member))

    def combine(k):
        own_slice(k).wait()
        pl.when(has_down)(pass_up(k, source_cut(k, 0, GROUP), 0, GROUP).wait_recv)
        pl.when(has_up)(pass_down(k, source_cut(k, 0, GROUP), 0, GROUP).wait_recv)

        def one_row(n, carry):
            first = start_of[n]
            weights = [weight_of[4 * n + a] for a in range(4)]
            for t in range(chunks[k][2] // LANES):
                at = pl.ds(t * LANES, LANES)
                total = weights[0] * source[k][first, :, at]
                for a in range(1, 4):
                    total = total + weights[a] * source[k][first + a, :, at]
                mixed[k][n, t] = total
            return carry

        lax.fori_loop(0, GROUP * rows, one_row, 0, unroll=4)
        for j in range(3):
            bring(j, k).start()
        keep(k).start()

    def chain(hop):
        if hop == 0:
            total = mine[...]
            for n in range(len(mates)):
                table_copy(n).wait_recv()
                total = total + met[n]
            plane[...] = total

            @pl.when(jnp.logical_not(has_down))
            def _():
                below[...] = jnp.zeros_like(below)

            @pl.when(jnp.logical_not(has_up))
            def _():
                above[...] = jnp.zeros_like(above)

        @pl.when(group == hop)
        def _():
            if hop > 0:
                up_copy.wait_recv()
            if hop < groups - 1:
                upward[...] = plane[...] + below[...]
                up_copy.start()

        @pl.when(group == groups - 1 - hop)
        def _():
            if hop > 0:
                down_copy.wait_recv()
            if hop < groups - 1:
                downward[...] = plane[...] + above[...]
                down_copy.start()

    def find_ratio():
        total = plane[...] + below[...] + above[...]
        for f in range(field_count):
            sums_at = total[f:f + 1, :]
            mass_before = jnp.sum(sums_at * total[field_count + 1:field_count + 2, :], axis=1, keepdims=True)
            mass_after = jnp.sum(sums_at * total[field_count:field_count + 1, :], axis=1, keepdims=True)
            ratio[f:f + 1, :] = jnp.broadcast_to(mass_before / mass_after, (1, LANES))

    def along_lon(f):
        for k in range(count):
            if chunks[k][0] == f:
                for j in range(3):
                    block = column_cut(position + steps[j], k)
                    remote(block, block, bring_send.at[j], bring_recv.at[j, k], {"lat": band}).wait_recv()
                keep(k).wait()
        lane = lax.broadcasted_iota(jnp.int32, (levels, LANES), 1)
        scale = jnp.broadcast_to(ratio[f:f + 1, :], (levels, LANES))

        def one_row(row, carry):
            for t in range(tiles):
                column[f][row, tiles + t] = column[f][row, t]
            column[f][row, 2 * tiles] = column[f][row, 0]
            lon = [lon_of[4 * row + n] * scale for n in range(4)]
            first = lax.rem(shift_ref[row] - 1 + lon_count, lon_count)
            rests = [lax.rem(first + n, LANES) for n in range(4)]
            turns = [lax.rem(LANES - rest, LANES) for rest in rests]
            stays = [lane < LANES - rest for rest in rests]
            bases = [(first + n) // LANES for n in range(4)]

            def turned(t):
                return [pltpu.roll(column[f][row, bases[n] + t], turns[n], 1) for n in range(4)]

            here = turned(0)
            for t in range(tiles):
                there = turned(t + 1)
                total = lon[0] * jnp.where(stays[0], here[0], there[0])
                for n in range(1, 4):
                    total = total + lon[n] * jnp.where(stays[n], here[n], there[n])
                moved_ref[row, f, :, pl.ds(t * LANES, LANES)] = total
                here = there
            return carry

        lax.fori_loop(0, rows, one_row, 0)

    pass_own(0)
    give_all(0)
    pass_own(1)
    for copy in scalars:
        copy.wait()
    for n in range(3):
        for j in range(3):
            note(n, j).start()
    load.wait()
    lane = lax.broadcasted_iota(jnp.int32, (1, mine.shape[1]), 1)
    taken = jnp.zeros(lane.shape, jnp.float32)
    for row in range(rows):
        departure = departure_of(
            departure_ref[row], extents_ref[0, 0], extents_ref[0, 1], first_row, rows, total_rows
        )
        lon_w = cubic(lon_t_ref[row])
        for n, weight in enumerate(lon_w):
            lon_of[4 * row + n] = weight
        share = area_ref[first_row + row] * (lon_w[0] + lon_w[1] + lon_w[2] + lon_w[3]) * (1.0 / levs)
        for a, weight in enumerate(cubic(lat_t_ref[row])):
            taken = taken + jnp.where(lane == departure - 1 + a, share * weight, 0.0)
    sums = [jnp.zeros(lane.shape, jnp.float32) for _ in range(field_count)]
    before = jnp.zeros(lane.shape, jnp.float32)
    for row in range(rows):
        before = before + jnp.where(lane == first_row + row, area_ref[first_row + row] * (1.0 / levs), 0.0)
        for f in range(field_count):
            total = jnp.sum(jnp.sum(held[row, f], axis=0, keepdims=True), axis=1, keepdims=True)
            sums[f] = sums[f] + jnp.where(lane == first_row + row, total, 0.0)
    mine[...] = jnp.zeros_like(mine)
    for f in range(field_count):
        mine[f:f + 1, :] = sums[f]
    mine[field_count:field_count + 1, :] = taken
    mine[field_count + 1:field_count + 2, :] = before
    for n in range(len(mates)):
        table_copy(n).start()

    for k in range(1, GIVEN):
        give_all(k)
    for k in range(count):
        own_slice(k).start()
    for k in range(PASSED):
        if k >= 2:
            pass_own(k)
        take(k)
    for row in range(rows):
        far_departure[position, row] = departure_ref[row]
        far_lat[position, row] = lat_t_ref[row]
    for e in range(2):
        far_extents[position, e] = extents_ref[0, e]
    for n in range(3):
        for j in range(3):
            note(n, j).wait_recv()
    for member in range(GROUP):
        member_row = (group * GROUP + member) * rows
        north, south = far_extents[member, 0], far_extents[member, 1]

        def prepare(row, carry):
            departure = departure_of(far_departure[member, row], north, south, member_row, rows, total_rows)
            start_of[member * rows + row] = departure - 1 - (group - 1) * GROUP * rows
            for a, weight in enumerate(cubic(far_lat[member, row])):
                weight_of[4 * (member * rows + row) + a] = weight
            return carry

        lax.fori_loop(0, rows, prepare, 0)
    chain(0)

    hop = 1
    finished = 0
    for k in range(count):
        give_all(k + GIVEN)
        pass_own(k + PASSED)
        take(k + PASSED)
        combine(k)
        while hop < groups and (hop * (count - WAIT)) // groups <= k:
            chain(hop)
            hop += 1
            if hop == groups:
                find_ratio()
        if k < count - 1 and hop == groups and chunks[k - WAIT][0] > finished:
            along_lon(finished)
            finished += 1
    for f in range(finished, field_count):
        along_lon(f)

    for k in range(count):
        for j in range(3):
            give(j, k).wait_send()
            bring(j, k).wait_send()
        pl.when(has_up)(pass_up(k, source_cut(k, 0, GROUP), 0, GROUP).wait_send)
        pl.when(has_down)(pass_down(k, source_cut(k, 0, GROUP), 0, GROUP).wait_send)
    for n in range(3):
        for j in range(3):
            note(n, j).wait_send()
    for n in range(len(mates)):
        table_copy(n).wait_send()
    pl.when(has_up)(up_copy.wait_send)
    pl.when(has_down)(down_copy.wait_send)


def advect(lat_t, lon_t, shift, departure_row, extents, area, fields):
    bands, levs = lax.axis_size("lat"), lax.axis_size("lev")
    rows, field_count, levels, lon_count = fields.shape
    table = (-(-(field_count + 2) // 8) * 8, -(-bands * rows // LANES) * LANES)
    mates = GROUP * levs - 1
    chunks = chunks_of(field_count, lon_count)
    count = len(chunks)
    dma = pltpu.SemaphoreType.DMA
    hbm = pl.BlockSpec(memory_space=pltpu.HBM)
    operands = (lat_t, lon_t, shift, departure_row, extents, area, fields)
    return pl.pallas_call(
        functools.partial(advect_kernel, bands, levs, chunks),
        out_shape=jax.ShapeDtypeStruct(fields.shape, fields.dtype),
        in_specs=[hbm] * 7,
        out_specs=pl.BlockSpec(memory_space=pltpu.VMEM),
        scratch_shapes=[
            pltpu.SMEM(lat_t.shape, jnp.float32),
            pltpu.SMEM(lon_t.shape, jnp.float32),
            pltpu.SMEM(shift.shape, jnp.int32),
            pltpu.SMEM(departure_row.shape, jnp.int32),
            pltpu.SMEM(extents.shape, jnp.int32),
            pltpu.SMEM(area.shape, jnp.float32),
            pltpu.VMEM(fields.shape, jnp.float32),
            pltpu.SMEM((GROUP, rows), jnp.int32),
            pltpu.SMEM((GROUP, 2), jnp.int32),
            pltpu.SMEM((GROUP, rows), jnp.float32),
            pltpu.SMEM((GROUP * rows,), jnp.int32),
            pltpu.SMEM((4 * GROUP * rows,), jnp.float32),
            pltpu.SMEM((4 * rows,), jnp.float32),
            pltpu.VMEM(table, jnp.float32),
            pltpu.VMEM((mates,) + table, jnp.float32),
        ]
        + [pltpu.VMEM(table, jnp.float32)] * 5
        + [
            pltpu.VMEM((table[0], LANES), jnp.float32),
            dma((6,)),
            dma,
            dma((3, 3)),
            dma((3, 3)),
            dma((3,)),
            dma((3, count)),
            dma((2,)),
            dma((2, count)),
            dma((count,)),
            dma((3,)),
            dma((3, count)),
            dma((count,)),
            dma((mates,)),
            dma((mates,)),
            dma((2,)),
            dma((2,)),
        ]
        + [pltpu.VMEM((3 * GROUP * rows, levels, size), jnp.float32) for _, _, size in chunks]
        + [pltpu.VMEM((GROUP * rows, size // LANES, levels, LANES), jnp.float32) for _, _, size in chunks]
        + [pltpu.VMEM((rows, 2 * lon_count // LANES + 1, levels, LANES), jnp.float32)] * field_count,
        compiler_params=pltpu.CompilerParams(
            collective_id=0, has_side_effects=True, vmem_limit_bytes=VMEM_BYTES
        ),
        name="advect",
    )(*[pltpu.with_memory_space_constraint(x, pltpu.HBM) for x in operands])


def per_device(fields, lat_fraction, lon_fraction, lon_shift, departure_row, extents):
    bands = lax.axis_size("lat")
    total_rows = bands * fields.shape[0]
    row_ids = np.arange(-(-total_rows // LANES) * LANES)
    area = np.where(row_ids < total_rows, np.cos(math.pi * (row_ids + 0.5) / total_rows - math.pi / 2.0), 0.0)
    area = jnp.asarray(area, jnp.float32)
    return advect(lat_fraction, lon_fraction, lon_shift, departure_row, extents, area, fields)


def solution(mesh):
    return jax.shard_map(
        per_device,
        mesh=mesh,
        in_specs=(
            P("lat", None, "lev", None),
            P("lat"),
            P("lat"),
            P("lat"),
            P("lat"),
            P("lat", None),
        ),
        out_specs=P("lat", None, "lev", None),
        check_vma=False,
    )
```

time: 79 us -> 69.1 us (0.87)
  Pallas kernels: 78.7 us -> 67.5 us
  local copies, waits for them, and re-layouts: 0 us -> 1.44 us
    pallas_call x2 -> x1, Pallas kernels: 78.7 us -> 67.5 us  [advect(): pl.pallas_call(functools.partial(advect_kernel, bands, levs, chunks), out...]
    unnamed x0 -> x1, local copies, waits for them, and re-layouts: none -> 1.44 us
where the time goes in v2:
time: 69.1 us; the launch traced here: 69 us
  Pallas kernels  67.5 us (98%)
  local copies, waits for them, and re-layouts  1.44 us (2%)
    pallas_call x1, Pallas kernels, advect(): pl.pallas_call(functools.partial(advect_kernel, bands, levs, chunks), out...  67.5 us
    unnamed x1, local copies, waits for them, and re-layouts  1.44 us

profile of v2, /device:TPU:0, one launch (start us, length us, event | category | flops | bytes accessed | tf_op | source)
XLA Modules:
  0.0 69.0 jit_solution(7040622306616404572)
XLA Ops:
  0.0 67.5 %advect.1 = f32[10,3,8,2560]{3,2,1,0:T(8,128)S(1)} custom-call(f32[10]{0:T(128)} %lat_t_hbm.1, f32[10]{0:T(128)} %lon_t_hbm.1, s32[10]{0:T(128)} %shift_hbm.1, s32[10]{0:T(128)} %departure_hbm.1, s32[1,2]{1,0:T(1,128)} %extents_hbm.1, f32[256]{0:T(256)} %constant.2.clone.area_hbm, f32[10,3,8,2560]{3,2,1,0:T(8,128)} %fields_ref.1), custom_call_target="tpu_custom_call" | custom-call | tf_op jit(solution)/shard_map/advect/pallas_call | solution.py:382
  67.5 1.4 %copy.9 = f32[10,3,8,2560]{3,2,1,0:T(8,128)} copy(f32[10,3,8,2560]{3,2,1,0:T(8,128)S(1)} %advect.1) | data formatting | bytes 4915200

commit v3 on v2

--- a/solution.py
+++ b/solution.py
@@ -12,9 +12,12 @@
 GROUP = 4
 LANES = 128
 PARTS = (3, 3, 3)
+TAIL = 4
 GIVEN = 4
 PASSED = 2
 WAIT = 1
+ROLL = 5
+OWN = 3
 VMEM_BYTES = 40 * 1024 * 1024
 MESH = pl.DeviceIdType.MESH
 
@@ -36,13 +39,19 @@
     return jnp.minimum(jnp.maximum(inside, 1), total_rows - 3)
 
 
+def tail_of(lon_count):
+    tiles = lon_count // LANES
+    return TAIL + (tiles - TAIL) % GROUP
+
+
 def chunks_of(field_count, lon_count):
-    tiles = lon_count // (GROUP * LANES)
     chunks = []
     for f in range(field_count):
+        last = f == field_count - 1
+        tiles = (lon_count // LANES - (tail_of(lon_count) if last else 0)) // GROUP
         parts = min(PARTS[min(f, len(PARTS) - 1)], tiles)
         edges = [tiles * n // parts for n in range(parts + 1)]
-        if f == field_count - 1:
+        if last:
             edges = [tiles - edge for edge in reversed(edges)]
         chunks += [(f, low * LANES, (high - low) * LANES) for low, high in zip(edges, edges[1:])]
     return chunks
@@ -50,18 +59,21 @@
 
 def advect_kernel(bands, levs, chunks, lat_t_hbm, lon_t_hbm, shift_hbm, departure_hbm, extents_hbm, area_hbm,
                   fields_ref, moved_ref, lat_t_ref, lon_t_ref, shift_ref, departure_ref, extents_ref,
-                  area_ref, held, far_departure, far_extents, far_lat, start_of, weight_of, lon_of, mine, met, plane,
+                  area_ref, held, far_departure, far_extents, far_lat, start_of, weight_of, lon_of, mine, pair, met, plane,
                   below, above, upward, downward, ratio, scalar_sem, load_sem, note_send, note_recv, give_send,
                   give_recv, pass_send, pass_recv, slice_sem, bring_send, bring_recv, keep_sem, table_send,
-                  table_recv, chain_send, chain_recv, *buffers):
+                  table_recv, chain_send, chain_recv, ready_sem,
+                  tail_at, tail_weight, tail_raw, tail_own, tail_up, tail_down, tail_below, tail_above, tail_give_send,
+                  tail_give_recv, tail_slice_sem, tail_send, tail_recv, *buffers):
     band, lev = lax.axis_index("lat"), lax.axis_index("lev")
     group, position = band // GROUP, lax.rem(band, GROUP)
     groups = bands // GROUP
     has_up = group < groups - 1
     has_down = group > 0
     rows, field_count, levels, lon_count = fields_ref.shape
-    width = lon_count // GROUP
     tiles = lon_count // LANES
+    tail = tail_of(lon_count)
+    last_field = field_count - 1
     count = len(chunks)
     source, mixed = buffers[:count], buffers[count:2 * count]
     column = buffers[2 * count:]
@@ -69,14 +81,15 @@
     step_one = 1 - 2 * lax.rem(position, 2)
     step_two = 2 - 4 * (position // 2)
     steps = [step_one, step_two, step_one + step_two]
-    mates = [{"lat": band + step, "lev": (lev + n) % levs} for n in range(levs) for step in [0] + steps][1:]
+    partner = {"lev": 1 - lev}
+    mates = [{"lat": band + step} for step in steps]
     up_peer, down_peer = {"lat": band + GROUP}, {"lat": band - GROUP}
 
     def signal(peer):
         pl.semaphore_signal(barrier, inc=1, device_id=peer, device_id_type=MESH)
 
     barrier = pltpu.get_barrier_semaphore()
-    for peer in mates:
+    for peer in [partner] + mates[:2]:
         signal(peer)
     pl.when(has_up)(lambda: signal(up_peer))
     pl.when(has_down)(lambda: signal(down_peer))
@@ -93,7 +106,7 @@
     load = pltpu.make_async_copy(fields_ref, held, load_sem)
     load.start()
 
-    pl.semaphore_wait(barrier, len(mates) + has_up.astype(jnp.int32) + has_down.astype(jnp.int32))
+    pl.semaphore_wait(barrier, 3 + has_up.astype(jnp.int32) + has_down.astype(jnp.int32))
 
     def remote(source_ref, target_ref, send_sem, recv_sem, peer):
         return pltpu.make_async_remote_copy(
@@ -101,8 +114,12 @@
             device_id=peer, device_id_type=MESH,
         )
 
+    def width_of(f):
+        return (lon_count - (tail * LANES if f == last_field else 0)) // GROUP
+
     def slice_at(home, k):
-        first, size = chunks[k][1:]
+        f, first, size = chunks[k]
+        width = width_of(f)
         return pl.ds(pl.multiple_of(home * width + first, LANES), size)
 
     def fields_cut(home, k):
@@ -113,11 +130,35 @@
 
     def column_cut(home, k):
         f, first, size = chunks[k]
-        return column[f].at[:, pl.ds((home * width + first) // LANES, size // LANES)]
+        return column[f].at[:, pl.ds((home * width_of(f) + first) // LANES, size // LANES)]
 
     def note(n, j):
         here, there = ((departure_ref, far_departure), (extents_ref.at[0], far_extents), (lat_t_ref, far_lat))[n]
-        return remote(here, there.at[position], note_send.at[n, j], note_recv.at[n, j], {"lat": band + steps[j]})
+        slot, peer = ([(position, mate) for mate in mates] + [(GROUP, up_peer), (GROUP + 1, down_peer)])[j]
+        return remote(here, there.at[slot], note_send.at[n, j], note_recv.at[n, j], peer)
+
+    def notes(j, act):
+        for n in range(3):
+            when_z(j - 3, getattr(note(n, j), act))
+
+    def when_z(j, body):
+        if j < 0:
+            body()
+        else:
+            pl.when((has_up, has_down)[j])(body)
+
+    def tail_cut():
+        return fields_ref.at[:, last_field, :, pl.ds((tiles - tail) * LANES, tail * LANES)]
+
+    def tail_block():
+        return tail_raw.at[pl.ds(position * rows, rows)]
+
+    def tail_give(j):
+        return remote(tail_cut(), tail_block(), tail_give_send.at[j], tail_give_recv.at[j], mates[j])
+
+    tail_slice = pltpu.make_async_copy(tail_cut(), tail_block(), tail_slice_sem)
+    tail_up_copy = remote(tail_up, tail_below, tail_send.at[0], tail_recv.at[0], up_peer)
+    tail_down_copy = remote(tail_down, tail_above, tail_send.at[1], tail_recv.at[1], down_peer)
 
     def give(j, k):
         home = position + steps[j]
@@ -151,15 +192,17 @@
         )
 
     def table_copy(n):
-        return remote(mine, met.at[n], table_send.at[n], table_recv.at[n], mates[n])
+        if n == 0:
+            return remote(mine, met.at[0], table_send.at[0], table_recv.at[0], partner)
+        return remote(pair, met.at[n], table_send.at[n], table_recv.at[n], mates[n - 1])
 
     up_copy = remote(upward, below, chain_send.at[0], chain_recv.at[0], up_peer)
     down_copy = remote(downward, above, chain_send.at[1], chain_recv.at[1], down_peer)
 
     def give_all(k):
-        if k < count:
+        if k <= count:
             for j in range(3):
-                give(j, k).start()
+                (give(j, k) if k < count else tail_give(j)).start()
 
     def pass_own(k):
         if k < count:
@@ -167,11 +210,77 @@
 
     def take(k):
         if k >= count:
+            if k == count:
+                tail_combine()
             return
         for j in range(3):
             give(j, k).wait_recv()
             member = position + steps[j]
             pass_on(k, member, source_cut(k, GROUP + member))
+
+    def tail_prepare(n, slot, member_row):
+        north, south = far_extents[slot, 0], far_extents[slot, 1]
+
+        def prepare(row, carry):
+            departure = departure_of(far_departure[slot, row], north, south, member_row, rows, total_rows)
+            for a, weight in enumerate(cubic(far_lat[slot, row])):
+                place = departure - 1 + a - group * GROUP * rows
+                inside = jnp.logical_and(place >= 0, place < GROUP * rows)
+                tail_at[4 * (n * rows + row) + a] = jnp.where(inside, place, 0)
+                tail_weight[4 * (n * rows + row) + a] = jnp.where(inside, weight, 0.0)
+            return carry
+
+        lax.fori_loop(0, rows, prepare, 0)
+
+    def tail_mix(n, target):
+        def one_row(row, carry):
+            places = [tail_at[4 * (n * rows + row) + a] for a in range(4)]
+            weights = [tail_weight[4 * (n * rows + row) + a] for a in range(4)]
+            for t in range(tail):
+                at = pl.ds(t * LANES, LANES)
+                total = weights[0] * tail_raw[places[0], :, at]
+                for a in range(1, 4):
+                    total = total + weights[a] * tail_raw[places[a], :, at]
+                target[row, t] = total
+            return carry
+
+        lax.fori_loop(0, rows, one_row, 0, unroll=2)
+
+    def tail_combine():
+        for j in range(3):
+            tail_give(j).wait_recv()
+        tail_slice.wait()
+
+        @pl.when(has_up)
+        def _():
+            tail_mix(2, tail_up)
+            tail_up_copy.start()
+
+        @pl.when(has_down)
+        def _():
+            tail_mix(1, tail_down)
+            tail_down_copy.start()
+
+        tail_mix(0, tail_own)
+
+        @pl.when(jnp.logical_not(has_down))
+        def _():
+            tail_below[...] = jnp.zeros_like(tail_below)
+
+        @pl.when(jnp.logical_not(has_up))
+        def _():
+            tail_above[...] = jnp.zeros_like(tail_above)
+
+    def tail_add():
+        pl.when(has_down)(tail_up_copy.wait_recv)
+        pl.when(has_up)(tail_down_copy.wait_recv)
+
+        def one_row(row, carry):
+            for t in range(tail):
+                column[last_field][row, tiles - tail + t] = tail_own[row, t] + tail_below[row, t] + tail_above[row, t]
+            return carry
+
+        lax.fori_loop(0, rows, one_row, 0, unroll=2)
 
     def combine(k):
         own_slice(k).wait()
@@ -196,8 +305,8 @@
 
     def chain(hop):
         if hop == 0:
-            total = mine[...]
-            for n in range(len(mates)):
+            total = pair[...]
+            for n in range(1, 4):
                 table_copy(n).wait_recv()
                 total = total + met[n]
             plane[...] = total
@@ -241,6 +350,8 @@
                     block = column_cut(position + steps[j], k)
                     remote(block, block, bring_send.at[j], bring_recv.at[j, k], {"lat": band}).wait_recv()
                 keep(k).wait()
+        if f == last_field:
+            tail_add()
         lane = lax.broadcasted_iota(jnp.int32, (levels, LANES), 1)
         scale = jnp.broadcast_to(ratio[f:f + 1, :], (levels, LANES))
 
@@ -268,16 +379,21 @@
                 here = there
             return carry
 
-        lax.fori_loop(0, rows, one_row, 0)
-
+        lax.fori_loop(0, rows, one_row, 0, unroll=ROLL)
+
+    pl.semaphore_signal(ready_sem, inc=1, device_id=mates[0], device_id_type=MESH)
     pass_own(0)
-    give_all(0)
-    pass_own(1)
+    for j in range(2):
+        give(j, 0).start()
+    for k in range(1, OWN):
+        pass_own(k)
+    pl.semaphore_wait(ready_sem, 1)
+    give(2, 0).start()
     for copy in scalars:
         copy.wait()
-    for n in range(3):
-        for j in range(3):
-            note(n, j).start()
+    for j in range(5):
+        notes(j, "start")
+    give_all(1)
     load.wait()
     lane = lax.broadcasted_iota(jnp.int32, (1, mine.shape[1]), 1)
     taken = jnp.zeros(lane.shape, jnp.float32)
@@ -303,16 +419,17 @@
         mine[f:f + 1, :] = sums[f]
     mine[field_count:field_count + 1, :] = taken
     mine[field_count + 1:field_count + 2, :] = before
-    for n in range(len(mates)):
-        table_copy(n).start()
-
-    for k in range(1, GIVEN):
-        give_all(k)
+    table_copy(0).start()
     for k in range(count):
         own_slice(k).start()
+    tail_slice.start()
+    table_copy(0).wait_recv()
+    pair[...] = mine[...] + met[0]
+    for n in range(1, 4):
+        table_copy(n).start()
+    for k in range(2, GIVEN):
+        give_all(k)
     for k in range(PASSED):
-        if k >= 2:
-            pass_own(k)
         take(k)
     for row in range(rows):
         far_departure[position, row] = departure_ref[row]
@@ -322,6 +439,8 @@
     for n in range(3):
         for j in range(3):
             note(n, j).wait_recv()
+        pl.when(has_down)(note(n, 3).wait_recv)
+        pl.when(has_up)(note(n, 4).wait_recv)
     for member in range(GROUP):
         member_row = (group * GROUP + member) * rows
         north, south = far_extents[member, 0], far_extents[member, 1]
@@ -335,12 +454,15 @@
 
         lax.fori_loop(0, rows, prepare, 0)
     chain(0)
+    tail_prepare(0, position, first_row)
+    pl.when(has_down)(lambda: tail_prepare(1, GROUP, first_row - GROUP * rows))
+    pl.when(has_up)(lambda: tail_prepare(2, GROUP + 1, first_row + GROUP * rows))
 
     hop = 1
     finished = 0
     for k in range(count):
         give_all(k + GIVEN)
-        pass_own(k + PASSED)
+        pass_own(k + OWN)
         take(k + PASSED)
         combine(k)
         while hop < groups and (hop * (count - WAIT)) // groups <= k:
@@ -360,11 +482,14 @@
             bring(j, k).wait_send()
         pl.when(has_up)(pass_up(k, source_cut(k, 0, GROUP), 0, GROUP).wait_send)
         pl.when(has_down)(pass_down(k, source_cut(k, 0, GROUP), 0, GROUP).wait_send)
-    for n in range(3):
-        for j in range(3):
-            note(n, j).wait_send()
-    for n in range(len(mates)):
+    for j in range(5):
+        notes(j, "wait_send")
+    for n in range(4):
         table_copy(n).wait_send()
+    for j in range(3):
+        tail_give(j).wait_send()
+    pl.when(has_up)(tail_up_copy.wait_send)
+    pl.when(has_down)(tail_down_copy.wait_send)
     pl.when(has_up)(up_copy.wait_send)
     pl.when(has_down)(down_copy.wait_send)
 
@@ -373,7 +498,8 @@
     bands, levs = lax.axis_size("lat"), lax.axis_size("lev")
     rows, field_count, levels, lon_count = fields.shape
     table = (-(-(field_count + 2) // 8) * 8, -(-bands * rows // LANES) * LANES)
-    mates = GROUP * levs - 1
+    tail = tail_of(lon_count)
+    tail_block = pltpu.VMEM((rows, tail, levels, LANES), jnp.float32)
     chunks = chunks_of(field_count, lon_count)
     count = len(chunks)
     dma = pltpu.SemaphoreType.DMA
@@ -392,22 +518,23 @@
             pltpu.SMEM(extents.shape, jnp.int32),
             pltpu.SMEM(area.shape, jnp.float32),
             pltpu.VMEM(fields.shape, jnp.float32),
-            pltpu.SMEM((GROUP, rows), jnp.int32),
-            pltpu.SMEM((GROUP, 2), jnp.int32),
-            pltpu.SMEM((GROUP, rows), jnp.float32),
+            pltpu.SMEM((GROUP + 2, rows), jnp.int32),
+            pltpu.SMEM((GROUP + 2, 2), jnp.int32),
+            pltpu.SMEM((GROUP + 2, rows), jnp.float32),
             pltpu.SMEM((GROUP * rows,), jnp.int32),
             pltpu.SMEM((4 * GROUP * rows,), jnp.float32),
             pltpu.SMEM((4 * rows,), jnp.float32),
             pltpu.VMEM(table, jnp.float32),
-            pltpu.VMEM((mates,) + table, jnp.float32),
+            pltpu.VMEM(table, jnp.float32),
+            pltpu.VMEM((4,) + table, jnp.float32),
         ]
         + [pltpu.VMEM(table, jnp.float32)] * 5
         + [
             pltpu.VMEM((table[0], LANES), jnp.float32),
             dma((6,)),
             dma,
-            dma((3, 3)),
-            dma((3, 3)),
+            dma((3, 5)),
+            dma((3, 5)),
             dma((3,)),
             dma((3, count)),
             dma((2,)),
@@ -416,8 +543,20 @@
             dma((3,)),
             dma((3, count)),
             dma((count,)),
-            dma((mates,)),
-            dma((mates,)),
+            dma((4,)),
+            dma((4,)),
+            dma((2,)),
+            dma((2,)),
+            pltpu.SemaphoreType.REGULAR,
+            pltpu.SMEM((12 * rows,), jnp.int32),
+            pltpu.SMEM((12 * rows,), jnp.float32),
+            pltpu.VMEM((GROUP * rows, levels, tail * LANES), jnp.float32),
+        ]
+        + [tail_block] * 5
+        + [
+            dma((3,)),
+            dma((3,)),
+            dma,
             dma((2,)),
             dma((2,)),
         ]

time: 69.1 us -> 67.1 us (0.971)
  Pallas kernels: 67.5 us -> 65.6 us
    pallas_call x1, Pallas kernels: 67.5 us -> 65.6 us  [advect(): pl.pallas_call(functools.partial(advect_kernel, bands, levs, chunks), out...]
where the time goes in v3:
time: 67.1 us; the launch traced here: 67 us
  Pallas kernels  65.6 us (98%)
  local copies, waits for them, and re-layouts  1.44 us (2%)
    pallas_call x1, Pallas kernels, advect(): pl.pallas_call(functools.partial(advect_kernel, bands, levs, chunks), out...  65.6 us
    unnamed x1, local copies, waits for them, and re-layouts  1.44 us

profile of v3, /device:TPU:0, one launch (start us, length us, event | category | flops | bytes accessed | tf_op | source)
XLA Modules:
  0.0 67.0 jit_solution(18328468387056089675)
XLA Ops:
  0.0 65.6 %advect.1 = f32[10,3,8,2560]{3,2,1,0:T(8,128)S(1)} custom-call(f32[10]{0:T(128)} %lat_t_hbm.1, f32[10]{0:T(128)} %lon_t_hbm.1, s32[10]{0:T(128)} %shift_hbm.1, s32[10]{0:T(128)} %departure_hbm.1, s32[1,2]{1,0:T(1,128)} %extents_hbm.1, f32[256]{0:T(256)} %constant.2.clone.area_hbm, f32[10,3,8,2560]{3,2,1,0:T(8,128)} %fields_ref.1), custom_call_target="tpu_custom_call" | custom-call | tf_op jit(solution)/shard_map/advect/pallas_call | solution.py:508
  65.6 1.4 %copy.9 = f32[10,3,8,2560]{3,2,1,0:T(8,128)} copy(f32[10,3,8,2560]{3,2,1,0:T(8,128)S(1)} %advect.1) | data formatting | bytes 4915200

commit v4 on v3

--- a/solution.py
+++ b/solution.py
@@ -11,13 +11,15 @@
 
 GROUP = 4
 LANES = 128
-PARTS = (3, 3, 3)
+PARTS = (2, 3, 3)
 TAIL = 4
-GIVEN = 4
-PASSED = 2
+GIVEN = 6
+PASSED = 3
 WAIT = 1
 ROLL = 5
 OWN = 3
+TAIL_GIVE = 0
+TAIL_RELAY = 2
 VMEM_BYTES = 40 * 1024 * 1024
 MESH = pl.DeviceIdType.MESH
 
@@ -150,13 +152,19 @@
     def tail_cut():
         return fields_ref.at[:, last_field, :, pl.ds((tiles - tail) * LANES, tail * LANES)]
 
-    def tail_block():
-        return tail_raw.at[pl.ds(position * rows, rows)]
+    def tail_block(member, first=0, size=None):
+        size = tail if size is None else size
+        return tail_raw.at[pl.ds(member * rows, rows), :, pl.ds(first * LANES, size * LANES)]
 
     def tail_give(j):
-        return remote(tail_cut(), tail_block(), tail_give_send.at[j], tail_give_recv.at[j], mates[j])
-
-    tail_slice = pltpu.make_async_copy(tail_cut(), tail_block(), tail_slice_sem)
+        if j < 2:
+            here, there = tail_cut(), tail_block(position)
+        else:
+            first = (0, tail // 2, tail)[j - 2:j]
+            here = there = tail_block(position + steps[j - 2], first[0], first[1] - first[0])
+        return remote(here, there, tail_give_send.at[j], tail_give_recv.at[j], mates[(0, 1, 1, 0)[j]])
+
+    tail_slice = pltpu.make_async_copy(tail_cut(), tail_block(position), tail_slice_sem)
     tail_up_copy = remote(tail_up, tail_below, tail_send.at[0], tail_recv.at[0], up_peer)
     tail_down_copy = remote(tail_down, tail_above, tail_send.at[1], tail_recv.at[1], down_peer)
 
@@ -200,9 +208,9 @@
     down_copy = remote(downward, above, chain_send.at[1], chain_recv.at[1], down_peer)
 
     def give_all(k):
-        if k <= count:
+        if k < count:
             for j in range(3):
-                (give(j, k) if k < count else tail_give(j)).start()
+                give(j, k).start()
 
     def pass_own(k):
         if k < count:
@@ -247,7 +255,7 @@
         lax.fori_loop(0, rows, one_row, 0, unroll=2)
 
     def tail_combine():
-        for j in range(3):
+        for j in range(2, 4):
             tail_give(j).wait_recv()
         tail_slice.wait()
 
@@ -464,6 +472,13 @@
         give_all(k + GIVEN)
         pass_own(k + OWN)
         take(k + PASSED)
+        if k == TAIL_GIVE:
+            for j in range(2):
+                tail_give(j).start()
+        if k == TAIL_RELAY:
+            for j in range(2):
+                tail_give(j).wait_recv()
+                tail_give(j + 2).start()
         combine(k)
         while hop < groups and (hop * (count - WAIT)) // groups <= k:
             chain(hop)
@@ -486,7 +501,7 @@
         notes(j, "wait_send")
     for n in range(4):
         table_copy(n).wait_send()
-    for j in range(3):
+    for j in range(4):
         tail_give(j).wait_send()
     pl.when(has_up)(tail_up_copy.wait_send)
     pl.when(has_down)(tail_down_copy.wait_send)
@@ -554,8 +569,8 @@
         ]
         + [tail_block] * 5
         + [
-            dma((3,)),
-            dma((3,)),
+            dma((4,)),
+            dma((4,)),
             dma,
             dma((2,)),
             dma((2,)),

time: 67.1 us -> 65.3 us (0.973)
  Pallas kernels: 65.6 us -> 63.7 us
    pallas_call x1, Pallas kernels: 65.6 us -> 63.7 us  [advect(): pl.pallas_call(functools.partial(advect_kernel, bands, levs, chunks), out...]
where the time goes in v4:
time: 65.3 us; the launch traced here: 65.1 us
  Pallas kernels  63.7 us (98%)
  local copies, waits for them, and re-layouts  1.44 us (2%)
    pallas_call x1, Pallas kernels, advect(): pl.pallas_call(functools.partial(advect_kernel, bands, levs, chunks), out...  63.7 us
    unnamed x1, local copies, waits for them, and re-layouts  1.44 us

profile of v4, /device:TPU:0, one launch (start us, length us, event | category | flops | bytes accessed | tf_op | source)
XLA Modules:
  0.0 65.1 jit_solution(17213668178688696547)
XLA Ops:
  0.0 63.7 %advect.1 = f32[10,3,8,2560]{3,2,1,0:T(8,128)S(1)} custom-call(f32[10]{0:T(128)} %lat_t_hbm.1, f32[10]{0:T(128)} %lon_t_hbm.1, s32[10]{0:T(128)} %shift_hbm.1, s32[10]{0:T(128)} %departure_hbm.1, s32[1,2]{1,0:T(1,128)} %extents_hbm.1, f32[256]{0:T(256)} %constant.2.clone.area_hbm, f32[10,3,8,2560]{3,2,1,0:T(8,128)} %fields_ref.1), custom_call_target="tpu_custom_call" | custom-call | tf_op jit(solution)/shard_map/advect/pallas_call | solution.py:523
  63.7 1.4 %copy.9 = f32[10,3,8,2560]{3,2,1,0:T(8,128)} copy(f32[10,3,8,2560]{3,2,1,0:T(8,128)S(1)} %advect.1) | data formatting | bytes 4915200

commit v5 on v4

--- a/solution.py
+++ b/solution.py
@@ -285,7 +285,9 @@
 
         def one_row(row, carry):
             for t in range(tail):
-                column[last_field][row, tiles - tail + t] = tail_own[row, t] + tail_below[row, t] + tail_above[row, t]
+                total = tail_own[row, t] + tail_below[row, t] + tail_above[row, t]
+                column[last_field][row, tiles - tail + t] = total
+                column[last_field][row, 2 * tiles - tail + t] = total
             return carry
 
         lax.fori_loop(0, rows, one_row, 0, unroll=2)
@@ -351,6 +353,16 @@
             mass_after = jnp.sum(sums_at * total[field_count:field_count + 1, :], axis=1, keepdims=True)
             ratio[f:f + 1, :] = jnp.broadcast_to(mass_before / mass_after, (1, LANES))
 
+    def repeat(f, places):
+        def one_row(row, carry):
+            for t in places:
+                column[f][row, tiles + t] = column[f][row, t]
+                if t == 0:
+                    column[f][row, 2 * tiles] = column[f][row, t]
+            return carry
+
+        lax.fori_loop(0, rows, one_row, 0, unroll=2)
+
     def along_lon(f):
         for k in range(count):
             if chunks[k][0] == f:
@@ -358,15 +370,15 @@
                     block = column_cut(position + steps[j], k)
                     remote(block, block, bring_send.at[j], bring_recv.at[j, k], {"lat": band}).wait_recv()
                 keep(k).wait()
+                first, size = chunks[k][1:]
+                starts = [(home * width_of(f) + first) // LANES for home in range(GROUP)]
+                repeat(f, [start + t for start in starts for t in range(size // LANES)])
         if f == last_field:
             tail_add()
         lane = lax.broadcasted_iota(jnp.int32, (levels, LANES), 1)
         scale = jnp.broadcast_to(ratio[f:f + 1, :], (levels, LANES))
 
         def one_row(row, carry):
-            for t in range(tiles):
-                column[f][row, tiles + t] = column[f][row, t]
-            column[f][row, 2 * tiles] = column[f][row, 0]
             lon = [lon_of[4 * row + n] * scale for n in range(4)]
             first = lax.rem(shift_ref[row] - 1 + lon_count, lon_count)
             rests = [lax.rem(first + n, LANES) for n in range(4)]
@@ -488,13 +500,9 @@
         if k < count - 1 and hop == groups and chunks[k - WAIT][0] > finished:
             along_lon(finished)
             finished += 1
-    for f in range(finished, field_count):
-        along_lon(f)
-
     for k in range(count):
         for j in range(3):
             give(j, k).wait_send()
-            bring(j, k).wait_send()
         pl.when(has_up)(pass_up(k, source_cut(k, 0, GROUP), 0, GROUP).wait_send)
         pl.when(has_down)(pass_down(k, source_cut(k, 0, GROUP), 0, GROUP).wait_send)
     for j in range(5):
@@ -503,10 +511,15 @@
         table_copy(n).wait_send()
     for j in range(4):
         tail_give(j).wait_send()
+    pl.when(has_up)(up_copy.wait_send)
+    pl.when(has_down)(down_copy.wait_send)
+    for f in range(finished, field_count):
+        along_lon(f)
+    for k in range(count):
+        for j in range(3):
+            bring(j, k).wait_send()
     pl.when(has_up)(tail_up_copy.wait_send)
     pl.when(has_down)(tail_down_copy.wait_send)
-    pl.when(has_up)(up_copy.wait_send)
-    pl.when(has_down)(down_copy.wait_send)
 
 
 def advect(lat_t, lon_t, shift, departure_row, extents, area, fields):

time: 65.3 us -> 65.1 us (level)
  no operation moved by 1% of the time
where the time goes in v5:
time: 65.1 us; the launch traced here: 64.9 us
  Pallas kernels  63.5 us (98%)
  local copies, waits for them, and re-layouts  1.44 us (2%)
    pallas_call x1, Pallas kernels, advect(): pl.pallas_call(functools.partial(advect_kernel, bands, levs, chunks), out...  63.5 us
    unnamed x1, local copies, waits for them, and re-layouts  1.44 us

profile of v5, /device:TPU:0, one launch (start us, length us, event | category | flops | bytes accessed | tf_op | source)
XLA Modules:
  0.0 64.9 jit_solution(15236991507739174022)
XLA Ops:
  0.0 63.5 %advect.1 = f32[10,3,8,2560]{3,2,1,0:T(8,128)S(1)} custom-call(f32[10]{0:T(128)} %lat_t_hbm.1, f32[10]{0:T(128)} %lon_t_hbm.1, s32[10]{0:T(128)} %shift_hbm.1, s32[10]{0:T(128)} %departure_hbm.1, s32[1,2]{1,0:T(1,128)} %extents_hbm.1, f32[256]{0:T(256)} %constant.2.clone.area_hbm, f32[10,3,8,2560]{3,2,1,0:T(8,128)} %fields_ref.1), custom_call_target="tpu_custom_call" | custom-call | tf_op jit(solution)/shard_map/advect/pallas_call | solution.py:536
  63.5 1.4 %copy.9 = f32[10,3,8,2560]{3,2,1,0:T(8,128)} copy(f32[10,3,8,2560]{3,2,1,0:T(8,128)S(1)} %advect.1) | data formatting | bytes 4915200

commit v6 on v5

--- a/solution.py
+++ b/solution.py
@@ -87,6 +87,11 @@
     mates = [{"lat": band + step} for step in steps]
     up_peer, down_peer = {"lat": band + GROUP}, {"lat": band - GROUP}
 
+    loads = [
+        pltpu.make_async_copy(fields_ref.at[:, f], held.at[:, f], load_sem.at[f]) for f in range(field_count)
+    ]
+    loads[0].start()
+
     def signal(peer):
         pl.semaphore_signal(barrier, inc=1, device_id=peer, device_id_type=MESH)
 
@@ -103,10 +108,8 @@
             (lon_t_hbm, lon_t_ref), (shift_hbm, shift_ref), (area_hbm, area_ref),
         ))
     ]
-    for copy in scalars:
+    for copy in scalars + loads[1:]:
         copy.start()
-    load = pltpu.make_async_copy(fields_ref, held, load_sem)
-    load.start()
 
     pl.semaphore_wait(barrier, 3 + has_up.astype(jnp.int32) + has_down.astype(jnp.int32))
 
@@ -125,7 +128,8 @@
         return pl.ds(pl.multiple_of(home * width + first, LANES), size)
 
     def fields_cut(home, k):
-        return fields_ref.at[:, chunks[k][0], :, slice_at(home, k)]
+        held_first = held if chunks[k][0] == 0 else fields_ref
+        return held_first.at[:, chunks[k][0], :, slice_at(home, k)]
 
     def source_cut(k, n, blocks=1):
         return source[k].at[pl.ds(n * rows, blocks * rows)]
@@ -365,6 +369,8 @@
 
     def along_lon(f):
         for k in range(count):
+            if f == last_field and k == count - 1:
+                tail_add()
             if chunks[k][0] == f:
                 for j in range(3):
                     block = column_cut(position + steps[j], k)
@@ -373,8 +379,6 @@
                 first, size = chunks[k][1:]
                 starts = [(home * width_of(f) + first) // LANES for home in range(GROUP)]
                 repeat(f, [start + t for start in starts for t in range(size // LANES)])
-        if f == last_field:
-            tail_add()
         lane = lax.broadcasted_iota(jnp.int32, (levels, LANES), 1)
         scale = jnp.broadcast_to(ratio[f:f + 1, :], (levels, LANES))
 
@@ -402,6 +406,7 @@
         lax.fori_loop(0, rows, one_row, 0, unroll=ROLL)
 
     pl.semaphore_signal(ready_sem, inc=1, device_id=mates[0], device_id_type=MESH)
+    loads[0].wait()
     pass_own(0)
     for j in range(2):
         give(j, 0).start()
@@ -414,7 +419,8 @@
     for j in range(5):
         notes(j, "start")
     give_all(1)
-    load.wait()
+    for copy in loads[1:]:
+        copy.wait()
     lane = lax.broadcasted_iota(jnp.int32, (1, mine.shape[1]), 1)
     taken = jnp.zeros(lane.shape, jnp.float32)
     for row in range(rows):
@@ -492,7 +498,7 @@
                 tail_give(j).wait_recv()
                 tail_give(j + 2).start()
         combine(k)
-        while hop < groups and (hop * (count - WAIT)) // groups <= k:
+        while hop < groups and (k == count - 1 if hop == groups - 1 else (hop * (count - WAIT)) // groups <= k):
             chain(hop)
             hop += 1
             if hop == groups:
@@ -560,7 +566,7 @@
         + [
             pltpu.VMEM((table[0], LANES), jnp.float32),
             dma((6,)),
-            dma,
+            dma((field_count,)),
             dma((3, 5)),
             dma((3, 5)),
             dma((3,)),

time: 65.1 us -> 64.8 us (level)
  no operation moved by 1% of the time
where the time goes in v6:
time: 64.8 us; the launch traced here: 64.7 us
  Pallas kernels  63.2 us (98%)
  local copies, waits for them, and re-layouts  1.44 us (2%)
    pallas_call x1, Pallas kernels, advect(): pl.pallas_call(functools.partial(advect_kernel, bands, levs, chunks), out...  63.2 us
    unnamed x1, local copies, waits for them, and re-layouts  1.44 us

profile of v6, /device:TPU:0, one launch (start us, length us, event | category | flops | bytes accessed | tf_op | source)
XLA Modules:
  0.0 64.7 jit_solution(12929460459373577515)
XLA Ops:
  0.0 63.2 %advect.1 = f32[10,3,8,2560]{3,2,1,0:T(8,128)S(1)} custom-call(f32[10]{0:T(128)} %lat_t_hbm.1, f32[10]{0:T(128)} %lon_t_hbm.1, s32[10]{0:T(128)} %shift_hbm.1, s32[10]{0:T(128)} %departure_hbm.1, s32[1,2]{1,0:T(1,128)} %extents_hbm.1, f32[256]{0:T(256)} %constant.2.clone.area_hbm, f32[10,3,8,2560]{3,2,1,0:T(8,128)} %fields_ref.1), custom_call_target="tpu_custom_call" | custom-call | tf_op jit(solution)/shard_map/advect/pallas_call | solution.py:542
  63.3 1.4 %copy.9 = f32[10,3,8,2560]{3,2,1,0:T(8,128)} copy(f32[10,3,8,2560]{3,2,1,0:T(8,128)S(1)} %advect.1) | data formatting | bytes 4915200

commit v7 on v6

--- a/solution.py
+++ b/solution.py
@@ -13,13 +13,13 @@
 LANES = 128
 PARTS = (2, 3, 3)
 TAIL = 4
-GIVEN = 6
+GIVEN = 5
 PASSED = 3
 WAIT = 1
 ROLL = 5
 OWN = 3
-TAIL_GIVE = 0
-TAIL_RELAY = 2
+TAIL_GIVE = 1
+TAIL_RELAY = 3
 VMEM_BYTES = 40 * 1024 * 1024
 MESH = pl.DeviceIdType.MESH
 
@@ -256,7 +256,7 @@
                 target[row, t] = total
             return carry
 
-        lax.fori_loop(0, rows, one_row, 0, unroll=2)
+        lax.fori_loop(0, rows, one_row, 0, unroll=5)
 
     def tail_combine():
         for j in range(2, 4):
@@ -294,7 +294,7 @@
                 column[last_field][row, 2 * tiles - tail + t] = total
             return carry
 
-        lax.fori_loop(0, rows, one_row, 0, unroll=2)
+        lax.fori_loop(0, rows, one_row, 0, unroll=5)
 
     def combine(k):
         own_slice(k).wait()
@@ -365,7 +365,7 @@
                     column[f][row, 2 * tiles] = column[f][row, t]
             return carry
 
-        lax.fori_loop(0, rows, one_row, 0, unroll=2)
+        lax.fori_loop(0, rows, one_row, 0, unroll=5)
 
     def along_lon(f):
         for k in range(count):

time: 64.8 us -> 64.8 us (level)
  no operation moved by 1% of the time
where the time goes in v7:
time: 64.8 us; the launch traced here: 64.7 us
  Pallas kernels  63.2 us (98%)
  local copies, waits for them, and re-layouts  1.44 us (2%)
    pallas_call x1, Pallas kernels, advect(): pl.pallas_call(functools.partial(advect_kernel, bands, levs, chunks), out...  63.2 us
    unnamed x1, local copies, waits for them, and re-layouts  1.44 us

profile of v7, /device:TPU:0, one launch (start us, length us, event | category | flops | bytes accessed | tf_op | source)
XLA Modules:
  0.0 64.7 jit_solution(1578088771001607449)
XLA Ops:
  0.0 63.2 %advect.1 = f32[10,3,8,2560]{3,2,1,0:T(8,128)S(1)} custom-call(f32[10]{0:T(128)} %lat_t_hbm.1, f32[10]{0:T(128)} %lon_t_hbm.1, s32[10]{0:T(128)} %shift_hbm.1, s32[10]{0:T(128)} %departure_hbm.1, s32[1,2]{1,0:T(1,128)} %extents_hbm.1, f32[256]{0:T(256)} %constant.2.clone.area_hbm, f32[10,3,8,2560]{3,2,1,0:T(8,128)} %fields_ref.1), custom_call_target="tpu_custom_call" | custom-call | tf_op jit(solution)/shard_map/advect/pallas_call | solution.py:542
  63.3 1.4 %copy.9 = f32[10,3,8,2560]{3,2,1,0:T(8,128)} copy(f32[10,3,8,2560]{3,2,1,0:T(8,128)S(1)} %advect.1) | data formatting | bytes 4915200
